TPU v7x, 32 devices: a whole 2x2x4 slice. The times are simulated.
32 devices in a mesh: band: 8 (over y, x, core), gblk: 4 (over z).
Axes of the slice: x: 2, y: 2, z: 4, core: 2. Of those that a mesh axis runs over, the one named last changes fastest.
Arguments:
- eps_inv: bfloat16 [2, 2, 8, 4, 512, 16384], P(None, None, None, 'gblk', None, 'band'), may hold values from -6 to 6
- pair_elements: bfloat16 [2, 1, 16, 16384], P(None, None, 'band'), may hold values from -0.046875 to 0.046875
Outputs:
- sigma_terms: float32 [2, 2, 1, 16], P(None, None, None, 'band')
All inputs are finite; a program needn't handle non-finite values.
Results may differ from a plain program's by a relative error of at most 0.0003.
Values may be sent and summed in bfloat16 or wider, within the bound.
No kernel may reach another device: no remote copies, remote signals or barrier semaphores. Data moves between devices by JAX's collectives and lax.ppermute only.
A program may use at most 128 MiB of HBM per device.

v0:
```python
import jax
import jax.numpy as jnp
from jax import lax
from jax.sharding import PartitionSpec as P


def shards(eps_inv, pair_elements):
    group_count = lax.axis_size("gblk")
    group_index = lax.axis_index("gblk")
    freqs = eps_inv.shape[0]
    rounds = eps_inv.shape[2]
    tile_rows = eps_inv.shape[4]
    width = eps_inv.shape[5]
    states = pair_elements.shape[1]
    local_bands = pair_elements.shape[2]
    columns = lax.all_to_all(pair_elements, "band", split_axis=3, concat_axis=2, tiled=True)
    all_bands = columns.shape[2]
    blocks = eps_inv.reshape(freqs, 2, -1, width)
    shaped = pair_elements.reshape(2, states, local_bands, rounds, group_count, tile_rows)
    picked = lax.dynamic_slice_in_dim(shaped, group_index, 1, 4)
    row_local = picked.reshape(2, states, local_bands, rounds * tile_rows)
    flat = columns.reshape(-1, width)
    contract_last = (((1,), (1,)), ((), ()))
    images = []
    for frequency in range(freqs):
        along_a = lax.dot_general(
            flat, blocks[frequency, 0], contract_last, preferred_element_type=jnp.float32
        )
        along_b = lax.dot_general(
            flat, blocks[frequency, 1], contract_last, preferred_element_type=jnp.float32
        )
        along_a = along_a.reshape(2, states, all_bands, -1)
        along_b = along_b.reshape(2, states, all_bands, -1)
        images.append(jnp.stack([along_a[0] - along_b[1], along_a[1] + along_b[0]]))
    image = jnp.stack(images)
    piece = lax.all_gather(row_local, "band", axis=2, tiled=True)
    real_part = piece[0].astype(jnp.float32)
    imag_part = piece[1].astype(jnp.float32)
    sigma_re = jnp.sum(real_part * image[:, 0] + imag_part * image[:, 1], axis=-1)
    sigma_im = jnp.sum(real_part * image[:, 1] - imag_part * image[:, 0], axis=-1)
    partial_sigma = jnp.stack([sigma_re, sigma_im], axis=1)
    reduced = lax.psum_scatter(partial_sigma, "band", scatter_dimension=3, tiled=True)
    return lax.psum(reduced, "gblk")


def solution(mesh):
    placed = (P(None, None, None, "gblk", None, "band"), P(None, None, "band", None))
    return jax.shard_map(
        shards, mesh=mesh, in_specs=placed, out_specs=P(None, None, None, "band"), check_vma=False
    )
```

profile of v0, /device:TPU:0, one launch (start us, length us, event | category | flops | bytes accessed | tf_op | source)
XLA Modules:
  0.0 138.5 jit_solution(16395664978475546550)
XLA Ops:
  0.0 0.0 copy-start.1
  0.0 0.0 copy-start
  0.0 15.4 %copy.24 = bf16[2,1,2,16384]{2,0,1,3:T(2,128)(2,1)} copy(bf16[2,1,2,16384]{3,2,1,0:T(2,128)(2,1)} %param.3) | data formatting | bytes 262144 | tf_op args[1]
  15.5 13.7 %reshape.124 = bf16[8,2,4096]{2,1,0:T(2,128)(2,1)} reshape(bf16[16384,1,2,2]{3,2,1,0:T(2,128)(2,1)} %bitcast.63) | data formatting | bytes 262144
  29.2 5.2 %all-to-all-start = ((bf16[8,2,4096]{2,1,0:T(2,128)(2,1)}), bf16[8,2,4096]{2,1,0:T(2,128)(2,1)S(1)}, u32[]{:S(2)}, u32[]{:S(2)}) async-start(bf16[8,2,4096]{2,1,0:T(2,128)(2,1)} %reshape.124), calls=%async_computation | async-start | bytes 262144 | tf_op jit(solution)/shard_map/all_to_all | solution.py:16
  34.4 0.0 copy-done
  34.4 0.1 reshape.113
  34.5 0.2 dynamic-slice_reduce_fusion
  34.8 9.8 %all_gather.3 = bf16[2,1,16,4096]{3,0,1,2:T(2,128)(2,1)S(1)} all-gather(bf16[2,1,2,4096]{3,0,1,2:T(2,128)(2,1)S(1)} %copy.23), channel_id=1, replica_groups=mesh['band'=8,'gblk'=4] {'band'}, dimensions={2}, use_global_device_ids=true | all-gather | bytes 294912 | tf_op jit(solution)/shard_map/all_gather | solution.py:36
  44.6 0.5 slice_convert_fusion.1
  45.1 0.3 copy_bitcast_fusion
  45.4 0.0 copy-done.1
  45.4 0.6 dynamic-slice
  46.7 0.0 all-to-all-done
  46.7 19.1 %reshape.125 = bf16[16384,1,2,2]{3,2,1,0:T(2,128)(2,1)} reshape(bf16[8,2,4096]{2,1,0:T(2,128)(2,1)S(1)} %all-to-all-done) | data formatting | bytes 262144
  65.8 11.9 %copy.29 = bf16[2,1,2,8,2048]{4,3,2,0,1:T(8,128)(2,1)S(1)} copy(bf16[2,1,2,8,2048]{2,0,4,3,1:T(2,128)(2,1)} %bitcast.62) | data formatting | bytes 262144 | tf_op jit(solution)/shard_map/all_to_all | solution.py:16
  77.6 0.1 copy.26
  77.8 0.1 reshape.115
  77.9 8.6 %fusion.2 = f32[32,4096]{1,0:T(8,128)S(1)} fusion(bf16[32,2048]{1,0:T(8,128)(2,1)S(1)} %reshape.115, bf16[2,2,4096,2048]{3,2,1,0:T(8,128)(2,1)} %bitcast.2), kind=kOutput, calls=%fused_computation.5 | convolution fusion | flops 536870912 | bytes 17432576 | tf_op jit(solution)/shard_map/dot_general | solution.py:29
  86.4 8.6 %fusion.3 = f32[32,4096]{1,0:T(8,128)S(1)} fusion(bf16[32,2048]{1,0:T(8,128)(2,1)S(1)} %reshape.115, bf16[2,2,4096,2048]{3,2,1,0:T(8,128)(2,1)} %bitcast.2), kind=kOutput, calls=%fused_computation.7 | convolution fusion | flops 536870912 | bytes 17432576 | tf_op jit(solution)/shard_map/dot_general | solution.py:26
  95.0 8.6 %fusion = f32[32,4096]{1,0:T(8,128)S(1)} fusion(bf16[32,2048]{1,0:T(8,128)(2,1)S(1)} %reshape.115, bf16[2,2,4096,2048]{3,2,1,0:T(8,128)(2,1)} %bitcast.2), kind=kOutput, calls=%fused_computation.1 | convolution fusion | flops 536870912 | bytes 17432576 | tf_op jit(solution)/shard_map/dot_general | solution.py:29
  103.6 8.6 %fusion.1 = f32[32,4096]{1,0:T(8,128)S(1)} fusion(bf16[32,2048]{1,0:T(8,128)(2,1)S(1)} %reshape.115, bf16[2,2,4096,2048]{3,2,1,0:T(8,128)(2,1)} %bitcast.2), kind=kOutput, calls=%fused_computation.3 | convolution fusion | flops 536870912 | bytes 17432576 | tf_op jit(solution)/shard_map/dot_general | solution.py:26
  112.2 0.1 fusion.10
  112.3 0.1 fusion.8
  112.4 0.2 add_reduce_fusion
  112.7 13.2 %all-reduce = f32[2,2,1,16]{3,0,2,1:T(2,128)S(1)} all-reduce(f32[2,2,1,16]{3,0,2,1:T(2,128)S(1)} %pad_maximum_fusion.1), channel_id=2, replica_groups=mesh['band'=8,'gblk'=4] {'band'}, use_global_device_ids=true, to_apply=%region_2.0.clone | all-reduce | flops 64 | bytes 512
  125.9 0.1 constant_dynamic-slice_fusion
  125.9 11.9 %psum.7 = f32[2,2,1,2]{3,0,2,1:T(2,128)S(1)} all-reduce(f32[2,2,1,2]{3,0,2,1:T(2,128)S(1)} %constant_dynamic-slice_fusion), channel_id=1, replica_groups=mesh['band'=8,'gblk'=4] {'gblk'}, use_global_device_ids=true, to_apply=%region_3.0 | all-reduce | flops 8 | bytes 64 | tf_op jit(solution)/shard_map/psum | solution.py:43
  137.9 0.6 copy.28
  (5 shorter events, 0.1 us)
Async XLA Ops:
  0.0 45.4 %copy-start.1 = (u32[32]{0:T(128)S(1)}, u32[32]{0:T(128)}, u32[]{:S(2)}) copy-start(u32[32]{0:T(128)} %constant.14) | copy-start | bytes 388
  0.0 34.4 %copy-start = (bf16[2,1,2,16384]{3,2,1,0:T(2,128)(2,1)S(1)}, bf16[2,1,2,16384]{3,2,1,0:T(2,128)(2,1)}, u32[]{:S(2)}) copy-start(bf16[2,1,2,16384]{3,2,1,0:T(2,128)(2,1)} %param.3) | copy-start | bytes 393220
  29.2 17.5 %all-to-all-start = ((bf16[8,2,4096]{2,1,0:T(2,128)(2,1)}), bf16[8,2,4096]{2,1,0:T(2,128)(2,1)S(1)}, u32[]{:S(2)}, u32[]{:S(2)}) async-start(bf16[8,2,4096]{2,1,0:T(2,128)(2,1)} %reshape.124), calls=%async_computation | async-start | bytes 262144 | tf_op jit(solution)/shard_map/all_to_all | solution.py:16
where the time goes:
time: 140 us; the launch traced here: 138 us
  local copies, waits for them, and re-layouts  62.2 us (44%)
  blocking collectives  35 us (25%)
  matrix products  34.3 us (24%)
  starting transfers between devices  5.2 us (4%)
    unnamed x10, local copies, waits for them, and re-layouts  49.2 us
    dot_general x2, matrix products, shards(): lax.dot_general(flat, blocks[frequency, 0], contract_last, preferred_elem...  17.2 us
    dot_general x2, matrix products, shards(): lax.dot_general(flat, blocks[frequency, 1], contract_last, preferred_elem...  17.1 us
    unnamed x1, blocking collectives  13.2 us
    all_to_all x2, local copies, waits for them, and re-layouts, shards(): lax.all_to_all(pair_elements, 'band', split_axis=3, concat_axis=2, tiled=...  12 us
    psum x1, blocking collectives, shards(): return lax.psum(reduced, 'gblk')  11.9 us
    all_gather x1, blocking collectives, shards(): piece = lax.all_gather(row_local, 'band', axis=2, tiled=True)  9.81 us
    all_to_all x1, starting transfers between devices, shards(): lax.all_to_all(pair_elements, 'band', split_axis=3, concat_axis=2, tiled=...  5.2 us
  transfers between devices with their start and end apart: 1, of which 0 were waited for; matrix products, arithmetic and copies ran while one was open for 1% of the time, Pallas kernels for 0%

commit v1 on v0

--- a/solution.py
+++ b/solution.py
@@ -2,6 +2,19 @@
 import jax.numpy as jnp
 from jax import lax
 from jax.sharding import PartitionSpec as P
+
+
+def lead_values_all(s0, dim_k, tile_in):
+    earlier, y = (s0.shape[:dim_k], s0.shape[dim_k + 1 :])
+    n_now = jnp.moveaxis(s0.reshape(*earlier, tile_in, -1, *y), dim_k, 0)
+    return n_now
+
+
+def stops_all_link(t0, row_dim):
+    t0 = jnp.moveaxis(t0, 0, row_dim)
+    inter = t0.shape
+    v_now = t0.reshape(*inter[:row_dim], inter[row_dim] * inter[row_dim + 1], *inter[row_dim + 2 :])
+    return v_now
 
 
 def shards(eps_inv, pair_elements):
@@ -13,7 +26,17 @@
     width = eps_inv.shape[5]
     states = pair_elements.shape[1]
     local_bands = pair_elements.shape[2]
-    columns = lax.all_to_all(pair_elements, "band", split_axis=3, concat_axis=2, tiled=True)
+    v1 = jax.lax.axis_size("band")
+    block_next = jax.lax.axis_index("band")
+    val, fresh = (v1, block_next)
+    mat_out = lead_values_all(pair_elements, 3, val)
+    pile = [mat_out[fresh]]
+    for kk in tuple(range(1, val)):
+        last = mat_out[fresh ^ kk]
+        passed = jax.lax.ppermute(last, axis_name="band", perm=[(no, no ^ kk) for no in range(val)])
+        pile.append(passed)
+    mat_out = jnp.stack(pile)[fresh ^ jnp.arange(val)]
+    columns = stops_all_link(mat_out, 2)
     all_bands = columns.shape[2]
     blocks = eps_inv.reshape(freqs, 2, -1, width)
     shaped = pair_elements.reshape(2, states, local_bands, rounds, group_count, tile_rows)

time: 140 us -> 87.5 us (0.62)
  local copies, waits for them, and re-layouts: 62.2 us -> 6.02 us
  waiting for transfers between devices: 0.01 us -> 2.79 us
  starting transfers between devices: 5.2 us -> 7.92 us
    unnamed x10 -> x17, local copies, waits for them, and re-layouts: 49.2 us -> 1.9 us
    all_to_all x2 -> x0, local copies, waits for them, and re-layouts: 12 us -> none  [shards(): lax.all_to_all(pair_elements, 'band', split_axis=3, concat_axis=2, tiled=...]
    ppermute x0 -> x7, starting transfers between devices: none -> 7.92 us  [shards(): jax.lax.ppermute(last, axis_name='band', perm=[(no, no ^ kk) for no in ra...]
    all_to_all x1 -> x0, starting transfers between devices: 5.2 us -> none  [shards(): lax.all_to_all(pair_elements, 'band', split_axis=3, concat_axis=2, tiled=...]
    ppermute x0 -> x7, waiting for transfers between devices: none -> 2.79 us  [shards(): jax.lax.ppermute(last, axis_name='band', perm=[(no, no ^ kk) for no in ra...]
  transfers between devices with their start and end apart: 1 -> 7, of which waited for: 0 -> 2; matrix products, arithmetic and copies ran while one was open for 1% -> 4% of each run, Pallas kernels for 0% -> 0%
where the time goes in v1:
time: 87.5 us; the launch traced here: 87.3 us
  blocking collectives  34.3 us (39%)
  matrix products  34.3 us (39%)
  starting transfers between devices  7.92 us (9%)
  local copies, waits for them, and re-layouts  6.02 us (7%)
  waiting for transfers between devices  2.79 us (3%)
  other arithmetic  1.02 us (1%)
  between operations  0.92 us (1%)
    dot_general x2, matrix products, shards(): lax.dot_general(flat, blocks[frequency, 0], contract_last, preferred_elem...  17.2 us
    dot_general x2, matrix products, shards(): lax.dot_general(flat, blocks[frequency, 1], contract_last, preferred_elem...  17.1 us
    unnamed x1, blocking collectives  13 us
    psum x1, blocking collectives, shards(): return lax.psum(reduced, 'gblk')  11.9 us
    all_gather x1, blocking collectives, shards(): piece = lax.all_gather(row_local, 'band', axis=2, tiled=True)  9.42 us
    ppermute x7, starting transfers between devices, shards(): jax.lax.ppermute(last, axis_name='band', perm=[(no, no ^ kk) for no in ra...  7.92 us
    ppermute x7, waiting for transfers between devices, shards(): jax.lax.ppermute(last, axis_name='band', perm=[(no, no ^ kk) for no in ra...  2.79 us
    unnamed x17, local copies, waits for them, and re-layouts  1.9 us
  transfers between devices with their start and end apart: 7, of which 2 were waited for; matrix products, arithmetic and copies ran while one was open for 4% of the time, Pallas kernels for 0%

profile of v1, /device:TPU:0, one launch (start us, length us, event | category | flops | bytes accessed | tf_op | source)
XLA Modules:
  0.0 87.3 jit_solution(11929376871455203752)
XLA Ops:
  0.0 1.0 %reshape.145 = bf16[2,1,2,8,2048]{4,3,2,0,1:T(8,128)(2,1)S(1)} reshape(bf16[2,1,2,16384]{3,2,1,0:T(2,128)(2,1)} %param.3) | data formatting | bytes 262144 | tf_op jit(solution)/shard_map/reshape | solution.py:9
  1.0 0.3 constant_dynamic-slice_fusion
  1.4 0.6 collective-permute-start
  2.0 2.6 %collective-permute-start.1 = (bf16[2,1,2,2048]{3,2,0,1:T(2,128)(2,1)S(1)}, bf16[2,1,2,2048]{3,2,0,1:T(2,128)(2,1)S(1)}, u32[]{:S(2)}, u32[]{:S(2)}) collective-permute-start(bf16[2,1,2,2048]{3,2,0,1:T(2,128)(2,1)S(1)} %bitcast.108), channel_id=1, source_target_pairs={{0,8},{4,12},{8,0},{12,4},{16,24},{20,28},{24,16},{28,20},{1,9},{5... | collective-permute-start | bytes 49160 | tf_op jit(solution)/shard_map/ppermute | solution.py:36
  4.5 0.2 collective-permute-start.2
  4.7 1.8 %collective-permute-start.3 = (bf16[2,1,2,2048]{3,2,0,1:T(2,128)(2,1)S(1)}, bf16[2,1,2,2048]{3,2,0,1:T(2,128)(2,1)S(1)}, u32[]{:S(2)}, u32[]{:S(2)}) collective-permute-start(bf16[2,1,2,2048]{3,2,0,1:T(2,128)(2,1)S(1)} %bitcast.106), channel_id=1, source_target_pairs={{0,16},{4,20},{8,24},{12,28},{16,0},{20,4},{24,8},{28,12},{1,17},{... | collective-permute-start | bytes 49160 | tf_op jit(solution)/shard_map/ppermute | solution.py:36
  6.6 0.1 collective-permute-start.4
  6.7 1.0 %reshape.143 = bf16[2,1,2,8,4,512]{5,4,3,2,0,1:T(4,128)(2,1)S(1)} reshape(bf16[2,1,2,16384]{3,2,1,0:T(2,128)(2,1)} %param.3) | data formatting | bytes 262144 | tf_op jit(solution)/shard_map/reshape | solution.py:42
  7.7 0.2 dynamic-slice_reduce_fusion
  8.0 9.4 %all_gather.3 = bf16[2,1,16,4096]{3,0,1,2:T(2,128)(2,1)S(1)} all-gather(bf16[2,1,2,4096]{3,0,1,2:T(2,128)(2,1)S(1)} %copy.18), channel_id=1, replica_groups=mesh['band'=8,'gblk'=4] {'band'}, dimensions={2}, use_global_device_ids=true | all-gather | bytes 294912 | tf_op jit(solution)/shard_map/all_gather | solution.py:59
  17.4 0.5 slice_convert_fusion.1
  17.9 0.3 copy_bitcast_fusion
  18.3 1.2 %dynamic-slice.32 = u32[1]{0:T(128)} dynamic-slice(u32[32]{0:T(128)} %constant.35, u32[]{:T(128)S(6)} %add.74), dynamic_slice_sizes={1} | dynamic-slice | bytes 12
  20.2 0.0 collective-permute-done
  20.2 1.5 %collective-permute-start.5 = (bf16[2,1,2,2048]{3,2,0,1:T(2,128)(2,1)S(1)}, bf16[2,1,2,2048]{3,2,0,1:T(2,128)(2,1)S(1)}, u32[]{:S(2)}, u32[]{:S(2)}) collective-permute-start(bf16[2,1,2,2048]{3,2,0,1:T(2,128)(2,1)S(1)} %bitcast.111), channel_id=1, source_target_pairs={{0,24},{4,28},{8,16},{12,20},{16,8},{20,12},{24,0},{28,4},{1,25},{... | collective-permute-start | bytes 49160 | tf_op jit(solution)/shard_map/ppermute | solution.py:36
  21.8 0.0 collective-permute-done.1
  21.8 1.2 %collective-permute-start.6 = (bf16[2,1,2,2048]{3,2,0,1:T(2,128)(2,1)S(1)}, bf16[2,1,2,2048]{3,2,0,1:T(2,128)(2,1)S(1)}, u32[]{:S(2)}, u32[]{:S(2)}) collective-permute-start(bf16[2,1,2,2048]{3,2,0,1:T(2,128)(2,1)S(1)} %bitcast.110), channel_id=1, source_target_pairs={{0,28},{4,24},{8,20},{12,16},{16,12},{20,8},{24,4},{28,0},{1,29},{... | collective-permute-start | bytes 49160 | tf_op jit(solution)/shard_map/ppermute | solution.py:36
  23.0 0.0 collective-permute-done.2
  23.1 0.0 collective-permute-done.3
  23.1 0.0 collective-permute-done.4
  23.1 1.8 %collective-permute-done.5 = bf16[2,1,2,2048]{3,2,0,1:T(2,128)(2,1)S(1)} collective-permute-done((bf16[2,1,2,2048]{3,2,0,1:T(2,128)(2,1)S(1)}, bf16[2,1,2,2048]{3,2,0,1:T(2,128)(2,1)S(1)}, u32[]{:S(2)}, u32[]{:S(2)}) %collective-permute-start.5) | collective-permute-done | bytes 16416 | tf_op jit(solution)/shard_map/ppermute | solution.py:36
  25.0 1.0 %collective-permute-done.6 = bf16[2,1,2,2048]{3,2,0,1:T(2,128)(2,1)S(1)} collective-permute-done((bf16[2,1,2,2048]{3,2,0,1:T(2,128)(2,1)S(1)}, bf16[2,1,2,2048]{3,2,0,1:T(2,128)(2,1)S(1)}, u32[]{:S(2)}, u32[]{:S(2)}) %collective-permute-start.6) | collective-permute-done | bytes 16416 | tf_op jit(solution)/shard_map/ppermute | solution.py:36
  26.0 0.8 gather_fusion
  26.8 0.1 copy.27
  26.9 0.1 reshape_reshape.3
  26.9 8.6 %fusion.2 = f32[32,4096]{1,0:T(8,128)S(1)} fusion(bf16[32,2048]{1,0:T(8,128)(2,1)S(1)} %reshape_reshape.3, bf16[2,2,4096,2048]{3,2,1,0:T(8,128)(2,1)} %bitcast.19), kind=kOutput, calls=%fused_computation.6 | convolution fusion | flops 536870912 | bytes 17432576 | tf_op jit(solution)/shard_map/dot_general | solution.py:52
  35.5 8.6 %fusion.3 = f32[32,4096]{1,0:T(8,128)S(1)} fusion(bf16[32,2048]{1,0:T(8,128)(2,1)S(1)} %reshape_reshape.3, bf16[2,2,4096,2048]{3,2,1,0:T(8,128)(2,1)} %bitcast.19), kind=kOutput, calls=%fused_computation.8 | convolution fusion | flops 536870912 | bytes 17432576 | tf_op jit(solution)/shard_map/dot_general | solution.py:49
  44.1 8.6 %fusion = f32[32,4096]{1,0:T(8,128)S(1)} fusion(bf16[32,2048]{1,0:T(8,128)(2,1)S(1)} %reshape_reshape.3, bf16[2,2,4096,2048]{3,2,1,0:T(8,128)(2,1)} %bitcast.19), kind=kOutput, calls=%fused_computation.2 | convolution fusion | flops 536870912 | bytes 17432576 | tf_op jit(solution)/shard_map/dot_general | solution.py:52
  52.7 8.6 %fusion.1 = f32[32,4096]{1,0:T(8,128)S(1)} fusion(bf16[32,2048]{1,0:T(8,128)(2,1)S(1)} %reshape_reshape.3, bf16[2,2,4096,2048]{3,2,1,0:T(8,128)(2,1)} %bitcast.19), kind=kOutput, calls=%fused_computation.4 | convolution fusion | flops 536870912 | bytes 17432576 | tf_op jit(solution)/shard_map/dot_general | solution.py:49
  61.2 0.1 fusion.10
  61.4 0.1 fusion.8
  61.5 0.2 add_reduce_fusion
  61.7 13.0 %all-reduce = f32[2,2,1,16]{3,0,2,1:T(2,128)S(1)} all-reduce(f32[2,2,1,16]{3,0,2,1:T(2,128)S(1)} %pad_maximum_fusion.1), channel_id=2, replica_groups=mesh['band'=8,'gblk'=4] {'band'}, use_global_device_ids=true, to_apply=%region_2.0.clone | all-reduce | flops 64 | bytes 512
  74.7 0.1 constant_dynamic-slice_fusion.8
  74.8 11.9 %psum.7 = f32[2,2,1,2]{3,0,2,1:T(2,128)S(1)} all-reduce(f32[2,2,1,2]{3,0,2,1:T(2,128)S(1)} %constant_dynamic-slice_fusion.8), channel_id=1, replica_groups=mesh['band'=8,'gblk'=4] {'gblk'}, use_global_device_ids=true, to_apply=%region_3.0 | all-reduce | flops 8 | bytes 64 | tf_op jit(solution)/shard_map/psum | solution.py:66
  86.7 0.6 copy.29
  (22 shorter events, 0.4 us)
Async XLA Ops:
  1.4 18.9 %collective-permute-start = (bf16[2,1,2,2048]{3,2,0,1:T(2,128)(2,1)S(1)}, bf16[2,1,2,2048]{3,2,0,1:T(2,128)(2,1)S(1)}, u32[]{:S(2)}, u32[]{:S(2)}) collective-permute-start(bf16[2,1,2,2048]{3,2,0,1:T(2,128)(2,1)S(1)} %bitcast.109), channel_id=1, source_target_pairs={{0,4},{4,0},{8,12},{12,8},{16,20},{20,16},{24,28},{28,24},{1,5},{5... | collective-permute-start | bytes 49160 | tf_op jit(solution)/shard_map/ppermute | solution.py:36
  2.0 19.8 %collective-permute-start.1 = (bf16[2,1,2,2048]{3,2,0,1:T(2,128)(2,1)S(1)}, bf16[2,1,2,2048]{3,2,0,1:T(2,128)(2,1)S(1)}, u32[]{:S(2)}, u32[]{:S(2)}) collective-permute-start(bf16[2,1,2,2048]{3,2,0,1:T(2,128)(2,1)S(1)} %bitcast.108), channel_id=1, source_target_pairs={{0,8},{4,12},{8,0},{12,4},{16,24},{20,28},{24,16},{28,20},{1,9},{5... | collective-permute-start | bytes 49160 | tf_op jit(solution)/shard_map/ppermute | solution.py:36
  4.5 18.5 %collective-permute-start.2 = (bf16[2,1,2,2048]{3,2,0,1:T(2,128)(2,1)S(1)}, bf16[2,1,2,2048]{3,2,0,1:T(2,128)(2,1)S(1)}, u32[]{:S(2)}, u32[]{:S(2)}) collective-permute-start(bf16[2,1,2,2048]{3,2,0,1:T(2,128)(2,1)S(1)} %bitcast.107), channel_id=1, source_target_pairs={{0,12},{4,8},{8,4},{12,0},{16,28},{20,24},{24,20},{28,16},{1,13},{... | collective-permute-start | bytes 49160 | tf_op jit(solution)/shard_map/ppermute | solution.py:36
  4.7 18.3 %collective-permute-start.3 = (bf16[2,1,2,2048]{3,2,0,1:T(2,128)(2,1)S(1)}, bf16[2,1,2,2048]{3,2,0,1:T(2,128)(2,1)S(1)}, u32[]{:S(2)}, u32[]{:S(2)}) collective-permute-start(bf16[2,1,2,2048]{3,2,0,1:T(2,128)(2,1)S(1)} %bitcast.106), channel_id=1, source_target_pairs={{0,16},{4,20},{8,24},{12,28},{16,0},{20,4},{24,8},{28,12},{1,17},{... | collective-permute-start | bytes 49160 | tf_op jit(solution)/shard_map/ppermute | solution.py:36
  6.6 16.5 %collective-permute-start.4 = (bf16[2,1,2,2048]{3,2,0,1:T(2,128)(2,1)S(1)}, bf16[2,1,2,2048]{3,2,0,1:T(2,128)(2,1)S(1)}, u32[]{:S(2)}, u32[]{:S(2)}) collective-permute-start(bf16[2,1,2,2048]{3,2,0,1:T(2,128)(2,1)S(1)} %bitcast.105), channel_id=1, source_target_pairs={{0,20},{4,16},{8,28},{12,24},{16,4},{20,0},{24,12},{28,8},{1,21},{... | collective-permute-start | bytes 49160 | tf_op jit(solution)/shard_map/ppermute | solution.py:36
  20.2 4.7 %collective-permute-start.5 = (bf16[2,1,2,2048]{3,2,0,1:T(2,128)(2,1)S(1)}, bf16[2,1,2,2048]{3,2,0,1:T(2,128)(2,1)S(1)}, u32[]{:S(2)}, u32[]{:S(2)}) collective-permute-start(bf16[2,1,2,2048]{3,2,0,1:T(2,128)(2,1)S(1)} %bitcast.111), channel_id=1, source_target_pairs={{0,24},{4,28},{8,16},{12,20},{16,8},{20,12},{24,0},{28,4},{1,25},{... | collective-permute-start | bytes 49160 | tf_op jit(solution)/shard_map/ppermute | solution.py:36
  21.8 4.1 %collective-permute-start.6 = (bf16[2,1,2,2048]{3,2,0,1:T(2,128)(2,1)S(1)}, bf16[2,1,2,2048]{3,2,0,1:T(2,128)(2,1)S(1)}, u32[]{:S(2)}, u32[]{:S(2)}) collective-permute-start(bf16[2,1,2,2048]{3,2,0,1:T(2,128)(2,1)S(1)} %bitcast.110), channel_id=1, source_target_pairs={{0,28},{4,24},{8,20},{12,16},{16,12},{20,8},{24,4},{28,0},{1,29},{... | collective-permute-start | bytes 49160 | tf_op jit(solution)/shard_map/ppermute | solution.py:36
